TPU v7x, 32 devices: a whole 2x2x4 slice. The times are simulated.
32 devices in a mesh: tm: 8 (over z, y), chan: 4 (over x, core).
Axes of the slice: x: 2, y: 2, z: 4, core: 2. Of those that a mesh axis runs over, the one named last changes fastest.
Arguments:
- series: float32 [256, 2048], P('chan', 'tm'), may hold values from -6 to 6
- lengths: int32 [16], replicated, may hold values from 42 to 128
Outputs:
- peak: float32 [2048], P('tm')
All inputs are finite; a program needn't handle non-finite values.
Results may differ from a plain program's by a relative error of at most 0.0015.
Values may be sent and summed in bfloat16 or wider, within the bound.
A program may use at most 128 MiB of HBM per device.

v0:
```python
import functools

import jax
import jax.numpy as jnp
from jax import lax
from jax.experimental import pallas as pl
from jax.experimental.pallas import tpu as pltpu
from jax.sharding import PartitionSpec as P

WIN = 256
STEPS = 2
GROUP = 16
EPS = 1e-05
MASKED = -1000000000.0
MESH = pl.DeviceIdType.MESH


def kernel(n_tm, n_chan, lengths, series, out, halo, xt, moments, mu, sc, z0, z1, z2, acc, recvbuf, peaks,
           halo_send, halo_recv, part_send, part_recv, peak_send, peak_recv):
    depth, rows = series.shape
    own = rows // n_chan
    total = rows * n_tm
    excl = WIN // 4
    block = lax.axis_index("tm")
    part = lax.axis_index("chan")

    def at(distance):
        return lax.rem(block + distance + n_tm, n_tm)

    def peer(d):
        return lax.rem(part + d, n_chan)

    barrier = pltpu.get_barrier_semaphore()
    greet = [(at(d), part) for d in (1, -1, -2)] + [(block, peer(d)) for d in range(1, n_chan)]
    for target in greet:
        pl.semaphore_signal(barrier, inc=1, device_id=target, device_id_type=MESH)
    pl.semaphore_wait(barrier, len(greet))

    halo_copies = []
    for slot, distance in enumerate((-1, 1, 2)):
        copy = pltpu.make_async_remote_copy(
            src_ref=series, dst_ref=halo.at[slot], send_sem=halo_send.at[slot], recv_sem=halo_recv.at[slot],
            device_id=(at(distance), part), device_id_type=MESH)
        copy.start()
        halo_copies.append(copy)

    half = WIN // 2
    reach = rows + half
    chunks = half // GROUP
    windows = (z0, z1, z2)

    def prepare(step):
        halo_copies[step].wait_recv()
        if step == 0:
            here, after = series[...], jnp.where(block == n_tm - 1, 0.0, halo[0])
        else:
            here, after = halo[step], series[...] if step == 1 else halo[1]
        x = jnp.concatenate([here, after], axis=1)
        xt[0:reach, :] = jnp.concatenate([x[:, :reach], x[:, half:half + reach]], axis=0).T
        span, source = 1, None
        while span < half:
            count = min(reach, -(-(reach - 2 * span) // 8) * 8)
            target = 0 if source is None else 1 - source
            mean_ref = xt if source is None else moments.at[source, 0]
            mean, later = mean_ref[0:count, :], mean_ref[span:span + count, :]
            gap = later - mean
            second = gap * gap * (span * 0.5)
            if source is not None:
                second = second + (moments[source, 1, 0:count, :] + moments[source, 1, span:span + count, :])
            moments[target, 0, 0:count, :] = (mean + later) * 0.5
            moments[target, 1, 0:count, :] = second
            span, source = 2 * span, target
        mean, second = moments[source, 0, 0:rows, :], moments[source, 1, 0:rows, :]
        later = pltpu.roll(mean, depth, 1)
        gap = later - mean
        second = second + pltpu.roll(second, depth, 1) + gap * gap * (half * 0.5)
        mu[...] = (mean + later) * 0.5
        sc[...] = lax.rsqrt(second * (1.0 / WIN) + EPS)

    def build(step, g):
        for tile in range(0, rows, 16):
            m, s = mu[tile:tile + 16, :], sc[tile:tile + 16, :]
            for k in range(GROUP):
                z = (xt[pl.ds(g * GROUP + (tile + k), 16), :] - m) * s
                windows[step][g, tile:tile + 16, 2 * depth * k:2 * depth * (k + 1)] = z.astype(jnp.bfloat16)

    def multiply(step, g):
        acc[step] += lax.dot_general(z0[g], windows[step][g], (((1,), (1,)), ((), ())),
                                     preferred_element_type=jnp.float32)

    def send(step):
        copies = []
        for d in range(1, n_chan):
            copy = pltpu.make_async_remote_copy(
                src_ref=acc.at[step, pl.ds(pl.multiple_of(peer(d) * own, own), own), :],
                dst_ref=recvbuf.at[step, d - 1],
                send_sem=part_send.at[step, d - 1], recv_sem=part_recv.at[step, d - 1],
                device_id=(block, peer(d)), device_id_type=MESH)
            copy.start()
            copies.append(copy)
        return copies

    acc[...] = jnp.zeros_like(acc)
    xt[reach:, :] = jnp.zeros((xt.shape[0] - reach, xt.shape[1]), jnp.float32)
    moments[:, :, reach:, :] = jnp.zeros((2, 2, xt.shape[0] - reach, xt.shape[1]), jnp.float32)
    sent = []
    for step in range(STEPS + 2):
        if step <= STEPS:
            prepare(step)

        def chunk(g, carry, step=step):
            if step > 0:
                multiply(step - 1, g)
            if step <= STEPS:
                build(step, g)
            return carry

        lax.fori_loop(0, chunks, chunk, 0)
        if step > 0:
            sent.append(send(step - 1))

    seg_len = rows // 2
    row_at = part * own + lax.broadcasted_iota(jnp.int32, (own, rows), 0)
    col_at = lax.broadcasted_iota(jnp.int32, (own, rows), 1)

    def valid(which, local):
        limit = jnp.where(local < seg_len, lengths[which * 2], lengths[which * 2 + 1])
        offset = jnp.where(local < seg_len, local, local - seg_len)
        return (offset < limit) & (which * rows + local <= total - WIN)

    rows_ok = valid(block, row_at)
    best = jnp.full((own, rows), MASKED, jnp.float32)
    for step in range(STEPS + 1):
        other = block - step
        safe = jnp.maximum(other, 0)
        keep = rows_ok & valid(safe, col_at) & (other >= 0) & (step * rows + row_at - col_at >= excl)
        summed = acc[step, pl.ds(pl.multiple_of(part * own, own), own), :]
        for d in range(1, n_chan):
            sent[step][d - 1].wait_recv()
            summed = summed + recvbuf[step, d - 1]
        best = jnp.maximum(best, jnp.where(keep, summed * (1.0 / WIN), MASKED))
    folded = best[:, :128]
    for at_lane in range(128, rows, 128):
        folded = jnp.maximum(folded, best[:, at_lane:at_lane + 128])
    top = jnp.max(folded.T, axis=0, keepdims=True)
    top = jnp.where(top > 0.5 * MASKED, top, 0.0)
    padded = jnp.concatenate([top, jnp.zeros((1, 128 - own), jnp.float32)], axis=1)
    peaks[0] = jnp.broadcast_to(padded, (8, 128))
    copies = []
    for d in range(1, n_chan):
        copy = pltpu.make_async_remote_copy(
            src_ref=peaks.at[0], dst_ref=peaks.at[d],
            send_sem=peak_send.at[d - 1], recv_sem=peak_recv.at[d - 1],
            device_id=(block, peer(d)), device_id_type=MESH)
        copy.start()
        copies.append(copy)
    for copy in copies:
        copy.wait_recv()
    slots = [peaks[d, 0:1, :own] for d in range(n_chan)]
    pieces = []
    for q in range(n_chan):
        piece = slots[0]
        for d in range(1, n_chan):
            piece = jnp.where(lax.rem(part + n_chan - d, n_chan) == q, slots[d], piece)
        pieces.append(piece)
    out[...] = jnp.concatenate(pieces, axis=1)

    for copy in halo_copies + [c for step in sent for c in step] + copies:
        copy.wait_send()


def solution(mesh):
    n_tm, n_chan = mesh.shape["tm"], mesh.shape["chan"]

    def body(series, lengths):
        depth, rows = series.shape
        own = rows // n_chan
        vmem = pl.BlockSpec(memory_space=pltpu.VMEM)
        peak = pl.pallas_call(
            functools.partial(kernel, n_tm, n_chan),
            out_shape=jax.ShapeDtypeStruct((1, rows), jnp.float32),
            in_specs=[pl.BlockSpec(memory_space=pltpu.SMEM), vmem],
            out_specs=vmem,
            scratch_shapes=[
                pltpu.VMEM((STEPS + 1, depth, rows), jnp.float32),
                pltpu.VMEM((rows + WIN // 2 + 16, 2 * depth), jnp.float32),
                pltpu.VMEM((2, 2, rows + WIN // 2 + 16, 2 * depth), jnp.float32),
                pltpu.VMEM((rows, 2 * depth), jnp.float32),
                pltpu.VMEM((rows, 2 * depth), jnp.float32),
                pltpu.VMEM((WIN // 2 // GROUP, rows, GROUP * 2 * depth), jnp.bfloat16),
                pltpu.VMEM((WIN // 2 // GROUP, rows, GROUP * 2 * depth), jnp.bfloat16),
                pltpu.VMEM((WIN // 2 // GROUP, rows, GROUP * 2 * depth), jnp.bfloat16),
                pltpu.VMEM((STEPS + 1, rows, rows), jnp.float32),
                pltpu.VMEM((STEPS + 1, n_chan - 1, own, rows), jnp.float32),
                pltpu.VMEM((n_chan, 8, 128), jnp.float32),
                pltpu.SemaphoreType.DMA((STEPS + 1,)),
                pltpu.SemaphoreType.DMA((STEPS + 1,)),
                pltpu.SemaphoreType.DMA((STEPS + 1, n_chan - 1)),
                pltpu.SemaphoreType.DMA((STEPS + 1, n_chan - 1)),
                pltpu.SemaphoreType.DMA((n_chan - 1,)),
                pltpu.SemaphoreType.DMA((n_chan - 1,)),
            ],
            compiler_params=pltpu.CompilerParams(collective_id=0, has_side_effects=True),
        )(lengths, series)
        return peak.reshape(rows)

    return jax.shard_map(
        body, mesh=mesh, in_specs=(P("chan", "tm"), P()), out_specs=P("tm"), check_vma=False)
```

profile of v0, /device:TPU:0, one launch (start us, length us, event | category | flops | bytes accessed | tf_op | source)
XLA Modules:
  0.0 35.6 jit_solution(842464393819819783)
XLA Ops:
  0.0 34.4 %shard_map.28 = f32[1,256]{1,0:T(1,128)} custom-call(s32[16]{0:T(128)} %lengths.1, f32[64,256]{1,0:T(8,128)} %series.1), custom_call_target="tpu_custom_call" | custom-call | tf_op jit(solution)/shard_map/pallas_call | solution.py:179
  34.4 0.0 copy-start
  34.4 0.7 %copy-done = f32[1,256]{1,0:T(1,128)S(1)} copy-done((f32[1,256]{1,0:T(1,128)S(1)}, f32[1,256]{1,0:T(1,128)}, u32[]{:S(2)}) %copy-start) | copy-done | bytes 1048
  35.1 0.6 %copy.4 = f32[256]{0:T(256)} copy(f32[256]{0:T(256)S(1)} %bitcast.1) | data formatting | bytes 2048
Async XLA Ops:
  34.4 0.7 %copy-start = (f32[1,256]{1,0:T(1,128)S(1)}, f32[1,256]{1,0:T(1,128)}, u32[]{:S(2)}) copy-start(f32[1,256]{1,0:T(1,128)} %shard_map.28) | copy-start | bytes 3076
where the time goes:
time: 35.8 us; the launch traced here: 35.6 us
  Pallas kernels  34.4 us (96%)
  local copies, waits for them, and re-layouts  1.22 us (3%)
    pallas_call x1, Pallas kernels, body(): pl.pallas_call(functools.partial(kernel, n_tm, n_chan), out_shape=jax.Sha...  34.4 us
    unnamed x3, local copies, waits for them, and re-layouts  1.22 us

commit v1 on v0

v1 whole, which is shorter than its diff:
```python
import functools

import jax
import jax.numpy as jnp
from jax import lax
from jax.experimental import pallas as pl
from jax.experimental.pallas import tpu as pltpu
from jax.sharding import PartitionSpec as P

WIN = 256
STEPS = 2
GROUP = 16
TILE = 32
EPS = 1e-05
MASKED = -1000000000.0
MESH = pl.DeviceIdType.MESH


def kernel(n_tm, n_chan, lengths, series, out, own_x, halo, xt, moments, mu, sc, z0e, z0o, ze, zo, acc,
           send16, recv32, recv16, peaks, load_sem, halo_send, halo_recv, part_send, part_recv, peak_send, peak_recv):
    depth, rows = own_x.shape
    total = rows * n_tm
    excl = WIN // 4
    half = WIN // 2
    lanes = 2 * depth
    chunks = half // GROUP
    heights = [rows - excl] + [rows] * STEPS
    block = lax.axis_index("tm")
    part = lax.axis_index("chan")

    def peer(d):
        return jnp.bitwise_xor(part, d)

    load = pltpu.make_async_copy(series, own_x, load_sem)
    load.start()

    barrier = pltpu.get_barrier_semaphore()
    for distance in (1, -1, -2):
        target = block + distance

        @pl.when((target >= 0) & (target < n_tm))
        def _(target=target):
            pl.semaphore_signal(barrier, inc=1, device_id=(target, part), device_id_type=MESH)

    for d in range(1, n_chan):
        pl.semaphore_signal(barrier, inc=1, device_id=(block, peer(d)), device_id_type=MESH)
    greeted = n_chan - 1
    for distance in (-1, 1, 2):
        target = block + distance
        greeted = greeted + jnp.where((target >= 0) & (target < n_tm), 1, 0)
    pl.semaphore_wait(barrier, greeted)

    reach = (-1, 1, 2)

    def halo_copy(slot):
        return pltpu.make_async_remote_copy(
            src_ref=series, dst_ref=halo.at[slot], send_sem=halo_send.at[slot], recv_sem=halo_recv.at[slot],
            device_id=(block + reach[slot], part), device_id_type=MESH)

    def sends(slot):
        target = block + reach[slot]
        return (target >= 0) & (target < n_tm)

    def receives(slot):
        origin = block - reach[slot]
        return (origin >= 0) & (origin < n_tm)

    def start_halo(slot):
        @pl.when(sends(slot))
        def _():
            halo_copy(slot).start()

    def sent_halo(slot):
        @pl.when(sends(slot))
        def _():
            halo_copy(slot).wait_send()

    def take_halo(slot):
        @pl.when(receives(slot))
        def _():
            halo_copy(slot).wait_recv()

    def place(value, at):
        xt[at:at + half, :] = jnp.concatenate([value[:, :half], value[:, half:]], axis=0).T

    def bridge(at):
        early, late = pltpu.roll(xt[at - half:at, :], depth, 1), pltpu.roll(xt[at + half:at + 2 * half, :], depth, 1)
        lane = lax.broadcasted_iota(jnp.int32, (half, lanes), 1)
        xt[at:at + half, :] = jnp.where(lane < depth, early, late)

    def base(step):
        return (STEPS - step) * rows

    def stats(step):
        lo = base(step)
        hi = lo + rows + (half if step == 0 else 0)
        span, level = 1, 0
        while span < half:
            last = min(hi, (STEPS + 2) * rows - half - 2 * span)
            last = lo + -(-(last - lo) // 8) * 8
            for at in range(lo, last, TILE):
                end = min(at + TILE, last)
                if span == 1:
                    here, later = xt[at:end, :], xt[at + span:end + span, :]
                else:
                    here, later = moments[level - 1, 0, at:end, :], moments[level - 1, 0, at + span:end + span, :]
                gap = later - here
                second = gap * gap * (0.5 / span)
                if span > 1:
                    second = second + (moments[level - 1, 1, at:end, :] + moments[level - 1, 1, at + span:end + span, :])
                moments[level, 0, at:end, :] = here + later
                moments[level, 1, at:end, :] = second
            span, level = 2 * span, level + 1
        for at in range(0, rows, TILE):
            here = moments[level - 1, 0, lo + at:lo + at + TILE, :]
            second = moments[level - 1, 1, lo + at:lo + at + TILE, :]
            later = pltpu.roll(here, depth, 1)
            gap = later - here
            second = second + pltpu.roll(second, depth, 1) + gap * gap * (0.5 / half)
            mu[step, at:at + TILE, :] = (here + later) * (1.0 / WIN)
            sc[step, at:at + TILE, :] = lax.rsqrt(second * (1.0 / WIN) + EPS)

    def build(step, g, target):
        for tile in range(0, rows, 16):
            m, s = mu[step, tile:tile + 16, :], sc[step, tile:tile + 16, :]
            for k in range(GROUP):
                z = (xt[pl.ds(base(step) + g * GROUP + (tile + k), 16), :] - m) * s
                target[k, tile:tile + 16, :] = z.astype(jnp.bfloat16)

    def product(step, weights, target):
        left = jnp.concatenate([target[k, 0:heights[step], :] for k in range(GROUP)], axis=1)
        right = jnp.concatenate([weights[k] for k in range(GROUP)], axis=1)
        return lax.dot_general(left, right, (((1,), (1,)), ((), ())), preferred_element_type=jnp.float32)

    def send(step):
        own = heights[step] // n_chan
        copies = []
        for d in range(1, n_chan):
            at = pl.ds(pl.multiple_of(peer(d) * own, own), own)
            if d == 1:
                src, dst = acc.at[step, at, :], recv32.at[step, 0:own, :]
            else:
                send16[step, d - 2, 0:own, :] = acc[step, at, :].astype(jnp.bfloat16)
                src, dst = send16.at[step, d - 2, 0:own, :], recv16.at[step, d - 2, 0:own, :]
            copy = pltpu.make_async_remote_copy(
                src_ref=src, dst_ref=dst, send_sem=part_send.at[step, d - 1], recv_sem=part_recv.at[step, d - 1],
                device_id=(block, peer(d)), device_id_type=MESH)
            copy.start()
            copies.append(copy)
        return copies

    start_halo(0)
    load.wait()
    place(own_x[...], STEPS * rows)
    pad = xt.shape[0] - ((STEPS + 2) * rows - half)
    xt[xt.shape[0] - pad:, :] = jnp.zeros((pad, lanes), jnp.float32)
    acc[...] = jnp.zeros_like(acc)
    sent_halo(0)
    start_halo(1)
    take_halo(0)
    start_halo(2)

    def arrive(step):
        if step == 0:
            place(jnp.where(block == n_tm - 1, 0.0, halo[0]), (STEPS + 1) * rows)
        else:
            take_halo(step)
            place(halo[step], base(step))
        bridge(base(step) + half)

    sent = []
    pairs = chunks // 2
    for step in range(STEPS + 1):
        arrive(step)
        stats(step)
        if step == 0:
            build(0, 0, z0e.at[0])
        else:
            build(step, 0, ze)

        def chunk(h, carry, step=step):
            first, second = (z0e.at[h], z0o.at[h]) if step == 0 else (ze, zo)
            a = product(step, z0e.at[h], first)
            build(step, 2 * h + 1, second)
            following = jnp.minimum(h + 1, pairs - 1)
            if step == 0:
                b = product(step, z0o.at[h], second)
                build(step, 2 * h + 2, z0e.at[h + 1])
            else:
                b = product(step, z0o.at[h], second)
                build(step, 2 * h + 2, ze)
            acc[step, 0:heights[step], :] += a + b
            return carry

        lax.fori_loop(0, pairs, chunk, 0)
        sent.append(send(step))

    lane_at = lax.broadcasted_iota(jnp.int32, (1, rows), 1)

    def valid(which, local):
        seg_len = rows // 2
        limit = jnp.where(local < seg_len, lengths[which * 2], lengths[which * 2 + 1])
        offset = jnp.where(local < seg_len, local, local - seg_len)
        return (offset < limit) & (which * rows + local <= total - WIN)

    best = None
    for step in range(STEPS + 1):
        own = heights[step] // n_chan
        row_at = part * own + lax.broadcasted_iota(jnp.int32, (own, rows), 0)
        other = block - step
        safe = jnp.maximum(other, 0)
        col_at = lax.broadcasted_iota(jnp.int32, (own, rows), 1)
        keep = valid(block, col_at) & valid(safe, row_at) & (other >= 0) & (step * rows + col_at - row_at >= excl)
        for copy in sent[step]:
            copy.wait_recv()
        summed = acc[step, pl.ds(pl.multiple_of(part * own, own), own), :] + recv32[step, 0:own, :]
        for d in range(2, n_chan):
            summed = summed + recv16[step, d - 2, 0:own, :].astype(jnp.float32)
        top = jnp.max(jnp.where(keep, summed * (1.0 / WIN), MASKED), axis=0, keepdims=True)
        best = top if best is None else jnp.maximum(best, top)
    peaks[0] = best
    copies = []
    for d in range(1, n_chan):
        copy = pltpu.make_async_remote_copy(
            src_ref=peaks.at[0], dst_ref=peaks.at[d], send_sem=peak_send.at[d - 1], recv_sem=peak_recv.at[d - 1],
            device_id=(block, peer(d)), device_id_type=MESH)
        copy.start()
        copies.append(copy)
    for copy in copies:
        copy.wait_recv()
    for d in range(1, n_chan):
        best = jnp.maximum(best, peaks[d])
    out[...] = jnp.where(best > 0.5 * MASKED, best, 0.0)

    sent_halo(1)
    sent_halo(2)
    for copy in [c for step in sent for c in step] + copies:
        copy.wait_send()


def solution(mesh):
    n_tm, n_chan = mesh.shape["tm"], mesh.shape["chan"]

    def body(series, lengths):
        depth, rows = series.shape
        half = WIN // 2
        lanes = 2 * depth
        pairs = half // GROUP // 2
        high = (STEPS + 2) * rows - half + 16 + GROUP
        levels = half.bit_length() - 1
        own = rows // n_chan
        vmem = pl.BlockSpec(memory_space=pltpu.VMEM)
        peak = pl.pallas_call(
            functools.partial(kernel, n_tm, n_chan),
            out_shape=jax.ShapeDtypeStruct((1, rows), jnp.float32),
            in_specs=[pl.BlockSpec(memory_space=pltpu.SMEM), pl.BlockSpec(memory_space=pl.ANY)],
            out_specs=vmem,
            scratch_shapes=[
                pltpu.VMEM((depth, rows), jnp.float32),
                pltpu.VMEM((STEPS + 1, depth, rows), jnp.float32),
                pltpu.VMEM((high, lanes), jnp.float32),
                pltpu.VMEM((levels, 2, high, lanes), jnp.float32),
                pltpu.VMEM((STEPS + 1, rows, lanes), jnp.float32),
                pltpu.VMEM((STEPS + 1, rows, lanes), jnp.float32),
                pltpu.VMEM((pairs + 1, GROUP, rows, lanes), jnp.bfloat16),
                pltpu.VMEM((pairs, GROUP, rows, lanes), jnp.bfloat16),
                pltpu.VMEM((GROUP, rows, lanes), jnp.bfloat16),
                pltpu.VMEM((GROUP, rows, lanes), jnp.bfloat16),
                pltpu.VMEM((STEPS + 1, rows, rows), jnp.float32),
                pltpu.VMEM((STEPS + 1, n_chan - 2, own, rows), jnp.bfloat16),
                pltpu.VMEM((STEPS + 1, own, rows), jnp.float32),
                pltpu.VMEM((STEPS + 1, n_chan - 2, own, rows), jnp.bfloat16),
                pltpu.VMEM((n_chan, 1, rows), jnp.float32),
                pltpu.SemaphoreType.DMA,
                pltpu.SemaphoreType.DMA((STEPS + 1,)),
                pltpu.SemaphoreType.DMA((STEPS + 1,)),
                pltpu.SemaphoreType.DMA((STEPS + 1, n_chan - 1)),
                pltpu.SemaphoreType.DMA((STEPS + 1, n_chan - 1)),
                pltpu.SemaphoreType.DMA((n_chan - 1,)),
                pltpu.SemaphoreType.DMA((n_chan - 1,)),
            ],
            compiler_params=pltpu.CompilerParams(collective_id=0, has_side_effects=True),
        )(lengths, series)
        return peak.reshape(rows)

    return jax.shard_map(
        body, mesh=mesh, in_specs=(P("chan", "tm"), P()), out_specs=P("tm"), check_vma=False)
```

time: 35.8 us -> 28.9 us (0.81)
  Pallas kernels: 34.4 us -> 27.6 us
    pallas_call x1, Pallas kernels: 34.4 us -> 27.6 us  [body(): pl.pallas_call(functools.partial(kernel, n_tm, n_chan), out_shape=jax.Sha...]
where the time goes in v1:
time: 28.9 us; the launch traced here: 28.8 us
  Pallas kernels  27.6 us (96%)
  local copies, waits for them, and re-layouts  1.22 us (4%)
    pallas_call x1, Pallas kernels, body(): pl.pallas_call(functools.partial(kernel, n_tm, n_chan), out_shape=jax.Sha...  27.6 us
    unnamed x3, local copies, waits for them, and re-layouts  1.22 us

profile of v1, /device:TPU:0, one launch (start us, length us, event | category | flops | bytes accessed | tf_op | source)
XLA Modules:
  0.0 28.8 jit_solution(17856240434238636617)
XLA Ops:
  0.0 27.6 %shard_map.28 = f32[1,256]{1,0:T(1,128)} custom-call(s32[16]{0:T(128)} %lengths.1, f32[64,256]{1,0:T(8,128)} %series.1), custom_call_target="tpu_custom_call" | custom-call | tf_op jit(solution)/shard_map/pallas_call | solution.py:253
  27.6 0.0 copy-start
  27.6 0.7 %copy-done = f32[1,256]{1,0:T(1,128)S(1)} copy-done((f32[1,256]{1,0:T(1,128)S(1)}, f32[1,256]{1,0:T(1,128)}, u32[]{:S(2)}) %copy-start) | copy-done | bytes 1048
  28.2 0.6 %copy.4 = f32[256]{0:T(256)} copy(f32[256]{0:T(256)S(1)} %bitcast.1) | data formatting | bytes 2048
Async XLA Ops:
  27.6 0.7 %copy-start = (f32[1,256]{1,0:T(1,128)S(1)}, f32[1,256]{1,0:T(1,128)}, u32[]{:S(2)}) copy-start(f32[1,256]{1,0:T(1,128)} %shard_map.28) | copy-start | bytes 3076

commit v2 on v1

--- a/solution.py
+++ b/solution.py
@@ -16,8 +16,8 @@
 MESH = pl.DeviceIdType.MESH
 
 
-def kernel(n_tm, n_chan, lengths, series, out, own_x, halo, xt, moments, mu, sc, z0e, z0o, ze, zo, acc,
-           send16, recv32, recv16, peaks, load_sem, halo_send, halo_recv, part_send, part_recv, peak_send, peak_recv):
+def kernel(n_tm, n_chan, lengths_in, series, out, lengths, own_x, halo, xt, moments, mu, sc, z0e, z0o, z1e, z1o, z2e, z2o,
+           acc, send16, recv32, recv16, peaks, load_sem, lengths_sem, halo_send, halo_recv, part_send, part_recv, peak_send, peak_recv):
     depth, rows = own_x.shape
     total = rows * n_tm
     excl = WIN // 4
@@ -33,6 +33,8 @@
 
     load = pltpu.make_async_copy(series, own_x, load_sem)
     load.start()
+    load_lengths = pltpu.make_async_copy(lengths_in, lengths, lengths_sem)
+    load_lengths.start()
 
     barrier = pltpu.get_barrier_semaphore()
     for distance in (1, -1, -2):
@@ -127,8 +129,9 @@
                 z = (xt[pl.ds(base(step) + g * GROUP + (tile + k), 16), :] - m) * s
                 target[k, tile:tile + 16, :] = z.astype(jnp.bfloat16)
 
-    def product(step, weights, target):
-        left = jnp.concatenate([target[k, 0:heights[step], :] for k in range(GROUP)], axis=1)
+    def product(weights, streamed):
+        left = jnp.concatenate(
+            [jnp.concatenate([z[k, 0:height, :] for z, height in streamed], axis=0) for k in range(GROUP)], axis=1)
         right = jnp.concatenate([weights[k] for k in range(GROUP)], axis=1)
         return lax.dot_general(left, right, (((1,), (1,)), ((), ())), preferred_element_type=jnp.float32)
 
@@ -164,38 +167,60 @@
         if step == 0:
             place(jnp.where(block == n_tm - 1, 0.0, halo[0]), (STEPS + 1) * rows)
         else:
-            take_halo(step)
+            if step == 1:
+                take_halo(step)
             place(halo[step], base(step))
         bridge(base(step) + half)
 
     sent = []
     pairs = chunks // 2
-    for step in range(STEPS + 1):
+    low, mid = heights[0], heights[0] + heights[1]
+
+    def add_near(value):
+        acc[0, 0:low, :] += value[:low]
+        acc[1, 0:heights[1], :] += value[low:mid]
+
+    for step in range(2):
         arrive(step)
         stats(step)
-        if step == 0:
-            build(0, 0, z0e.at[0])
-        else:
-            build(step, 0, ze)
-
-        def chunk(h, carry, step=step):
-            first, second = (z0e.at[h], z0o.at[h]) if step == 0 else (ze, zo)
-            a = product(step, z0e.at[h], first)
-            build(step, 2 * h + 1, second)
-            following = jnp.minimum(h + 1, pairs - 1)
-            if step == 0:
-                b = product(step, z0o.at[h], second)
-                build(step, 2 * h + 2, z0e.at[h + 1])
-            else:
-                b = product(step, z0o.at[h], second)
-                build(step, 2 * h + 2, ze)
-            acc[step, 0:heights[step], :] += a + b
-            return carry
-
-        lax.fori_loop(0, pairs, chunk, 0)
-        sent.append(send(step))
-
-    lane_at = lax.broadcasted_iota(jnp.int32, (1, rows), 1)
+        build(step, 0, z0e.at[0] if step == 0 else z1e)
+
+    def near(h, carry):
+        first = product(z0e.at[h], [(z0e.at[h], low), (z1e, heights[1])])
+        build(0, 2 * h + 1, z0o.at[h])
+        build(1, 2 * h + 1, z1o)
+        second = product(z0o.at[h], [(z0o.at[h], low), (z1o, heights[1])])
+        build(0, 2 * h + 2, z0e.at[h + 1])
+        build(1, 2 * h + 2, z1e)
+        add_near(first + second)
+        return carry
+
+    lax.fori_loop(0, pairs - 1, near, 0)
+    take_halo(2)
+    last = pairs - 1
+    first = product(z0e.at[last], [(z0e.at[last], low), (z1e, heights[1])])
+    build(0, 2 * last + 1, z0o.at[last])
+    build(1, 2 * last + 1, z1o)
+    second = product(z0o.at[last], [(z0o.at[last], low), (z1o, heights[1])])
+    arrive(2)
+    stats(2)
+    build(2, 0, z2e)
+    add_near(first + second)
+    sent.append(send(0))
+    sent.append(send(1))
+
+    def far(h, carry):
+        first = product(z0e.at[h], [(z2e, heights[2])])
+        build(2, 2 * h + 1, z2o)
+        second = product(z0o.at[h], [(z2o, heights[2])])
+        build(2, 2 * h + 2, z2e)
+        acc[2] += first + second
+        return carry
+
+    lax.fori_loop(0, pairs, far, 0)
+    sent.append(send(2))
+
+    load_lengths.wait()
 
     def valid(which, local):
         seg_len = rows // 2
@@ -252,10 +277,11 @@
         vmem = pl.BlockSpec(memory_space=pltpu.VMEM)
         peak = pl.pallas_call(
             functools.partial(kernel, n_tm, n_chan),
-            out_shape=jax.ShapeDtypeStruct((1, rows), jnp.float32),
-            in_specs=[pl.BlockSpec(memory_space=pltpu.SMEM), pl.BlockSpec(memory_space=pl.ANY)],
+            out_shape=pltpu.VMEM((1, rows), jnp.float32),
+            in_specs=[pl.BlockSpec(memory_space=pl.ANY), pl.BlockSpec(memory_space=pl.ANY)],
             out_specs=vmem,
             scratch_shapes=[
+                pltpu.SMEM(lengths.shape, jnp.int32),
                 pltpu.VMEM((depth, rows), jnp.float32),
                 pltpu.VMEM((STEPS + 1, depth, rows), jnp.float32),
                 pltpu.VMEM((high, lanes), jnp.float32),
@@ -266,11 +292,14 @@
                 pltpu.VMEM((pairs, GROUP, rows, lanes), jnp.bfloat16),
                 pltpu.VMEM((GROUP, rows, lanes), jnp.bfloat16),
                 pltpu.VMEM((GROUP, rows, lanes), jnp.bfloat16),
+                pltpu.VMEM((GROUP, rows, lanes), jnp.bfloat16),
+                pltpu.VMEM((GROUP, rows, lanes), jnp.bfloat16),
                 pltpu.VMEM((STEPS + 1, rows, rows), jnp.float32),
                 pltpu.VMEM((STEPS + 1, n_chan - 2, own, rows), jnp.bfloat16),
                 pltpu.VMEM((STEPS + 1, own, rows), jnp.float32),
                 pltpu.VMEM((STEPS + 1, n_chan - 2, own, rows), jnp.bfloat16),
                 pltpu.VMEM((n_chan, 1, rows), jnp.float32),
+                pltpu.SemaphoreType.DMA,
                 pltpu.SemaphoreType.DMA,
                 pltpu.SemaphoreType.DMA((STEPS + 1,)),
                 pltpu.SemaphoreType.DMA((STEPS + 1,)),

time: 28.9 us -> 25.1 us (0.87)
  the two profiles are of different devices: /device:TPU:0 before, /device:TPU:19 now
where the time goes in v2:
time: 25.1 us; the launch traced here: 25 us
  Pallas kernels  24.4 us (97%)
  local copies, waits for them, and re-layouts  0.56 us (2%)
    pallas_call x1, Pallas kernels, body(): pl.pallas_call(functools.partial(kernel, n_tm, n_chan), out_shape=pltpu.V...  24.4 us
    unnamed x1, local copies, waits for them, and re-layouts  0.56 us

profile of v2, /device:TPU:19, one launch (start us, length us, event | category | flops | bytes accessed | tf_op | source)
XLA Modules:
  0.0 25.0 jit_solution(17757233732435717705)
XLA Ops:
  0.0 24.4 %shard_map.28 = f32[1,256]{1,0:T(1,128)S(1)} custom-call(s32[16]{0:T(128)} %lengths_in.1, f32[64,256]{1,0:T(8,128)} %series.1), custom_call_target="tpu_custom_call" | custom-call | tf_op jit(solution)/shard_map/pallas_call | solution.py:278
  24.4 0.6 %copy.4 = f32[256]{0:T(256)} copy(f32[256]{0:T(256)S(1)} %bitcast.1) | data formatting | bytes 2048

commit v3 on v2

--- a/solution.py
+++ b/solution.py
@@ -11,6 +11,7 @@
 STEPS = 2
 GROUP = 16
 TILE = 32
+EARLY = 2
 EPS = 1e-05
 MASKED = -1000000000.0
 MESH = pl.DeviceIdType.MESH
@@ -56,7 +57,7 @@
 
     def halo_copy(slot):
         return pltpu.make_async_remote_copy(
-            src_ref=series, dst_ref=halo.at[slot], send_sem=halo_send.at[slot], recv_sem=halo_recv.at[slot],
+            src_ref=own_x, dst_ref=halo.at[slot], send_sem=halo_send.at[slot], recv_sem=halo_recv.at[slot],
             device_id=(block + reach[slot], part), device_id_type=MESH)
 
     def sends(slot):
@@ -82,13 +83,8 @@
         def _():
             halo_copy(slot).wait_recv()
 
-    def place(value, at):
-        xt[at:at + half, :] = jnp.concatenate([value[:, :half], value[:, half:]], axis=0).T
-
-    def bridge(at):
-        early, late = pltpu.roll(xt[at - half:at, :], depth, 1), pltpu.roll(xt[at + half:at + 2 * half, :], depth, 1)
-        lane = lax.broadcasted_iota(jnp.int32, (half, lanes), 1)
-        xt[at:at + half, :] = jnp.where(lane < depth, early, late)
+    def place(upper, lower, at):
+        xt[at:at + half, :] = jnp.concatenate([upper, lower], axis=0).T
 
     def base(step):
         return (STEPS - step) * rows
@@ -138,7 +134,7 @@
     def send(step):
         own = heights[step] // n_chan
         copies = []
-        for d in range(1, n_chan):
+        for d in [*range(2, n_chan), 1]:
             at = pl.ds(pl.multiple_of(peer(d) * own, own), own)
             if d == 1:
                 src, dst = acc.at[step, at, :], recv32.at[step, 0:own, :]
@@ -152,72 +148,90 @@
             copies.append(copy)
         return copies
 
+    load.wait()
     start_halo(0)
-    load.wait()
-    place(own_x[...], STEPS * rows)
+    place(own_x[:, :half], own_x[:, half:], base(0))
     pad = xt.shape[0] - ((STEPS + 2) * rows - half)
     xt[xt.shape[0] - pad:, :] = jnp.zeros((pad, lanes), jnp.float32)
     acc[...] = jnp.zeros_like(acc)
     sent_halo(0)
     start_halo(1)
+    start_halo(2)
     take_halo(0)
-    start_halo(2)
 
     def arrive(step):
         if step == 0:
-            place(jnp.where(block == n_tm - 1, 0.0, halo[0]), (STEPS + 1) * rows)
+            early, late = own_x, jnp.where(block == n_tm - 1, 0.0, halo[0])
+            place(late[:, :half], late[:, half:], base(0) + rows)
+            place(early[:, half:], late[:, :half], base(0) + half)
         else:
-            if step == 1:
-                take_halo(step)
-            place(halo[step], base(step))
-        bridge(base(step) + half)
+            early, late = halo[step], own_x if step == 1 else halo[1]
+            place(early[:, :half], early[:, half:], base(step))
+            place(early[:, half:], late[:, :half], base(step) + half)
 
     sent = []
     pairs = chunks // 2
     low, mid = heights[0], heights[0] + heights[1]
 
-    def add_near(value):
-        acc[0, 0:low, :] += value[:low]
-        acc[1, 0:heights[1], :] += value[low:mid]
+    take = (low, heights[1], heights[2])
+
+    def near(weights, mine, previous):
+        return product(weights, [(mine, take[0]), (previous, take[1])])
 
     for step in range(2):
+        if step == 1:
+            take_halo(1)
         arrive(step)
         stats(step)
         build(step, 0, z0e.at[0] if step == 0 else z1e)
-
-    def near(h, carry):
-        first = product(z0e.at[h], [(z0e.at[h], low), (z1e, heights[1])])
+    take_halo(2)
+
+    def add_near(first, second, fresh=False):
+        for step, lo, hi in ((0, 0, low), (1, low, mid)):
+            value = first[lo:hi] + second[lo:hi]
+            acc[step, 0:hi - lo, :] = value if fresh else acc[step, 0:hi - lo, :] + value
+
+    for h in range(EARLY):
+        first = near(z0e.at[h], z0e.at[h], z1e)
         build(0, 2 * h + 1, z0o.at[h])
         build(1, 2 * h + 1, z1o)
-        second = product(z0o.at[h], [(z0o.at[h], low), (z1o, heights[1])])
+        if h == 0:
+            arrive(2)
+        second = near(z0o.at[h], z0o.at[h], z1o)
         build(0, 2 * h + 2, z0e.at[h + 1])
         build(1, 2 * h + 2, z1e)
-        add_near(first + second)
+        if h == 0:
+            stats(2)
+        if h == EARLY - 1:
+            build(2, 2 * h + 2, z2e)
+        add_near(first, second, h == 0)
+
+    def every(h, carry):
+        first = product(z0e.at[h], [(z0e.at[h], take[0]), (z1e, take[1]), (z2e, take[2])])
+        build(0, 2 * h + 1, z0o.at[h])
+        build(1, 2 * h + 1, z1o)
+        build(2, 2 * h + 1, z2o)
+        second = product(z0o.at[h], [(z0o.at[h], take[0]), (z1o, take[1]), (z2o, take[2])])
+        build(0, 2 * h + 2, z0e.at[h + 1])
+        build(1, 2 * h + 2, z1e)
+        build(2, lax.rem(2 * h + 2, chunks), z2e)
+        add_near(first, second)
+        acc[2] += first[mid:] + second[mid:]
         return carry
 
-    lax.fori_loop(0, pairs - 1, near, 0)
-    take_halo(2)
-    last = pairs - 1
-    first = product(z0e.at[last], [(z0e.at[last], low), (z1e, heights[1])])
-    build(0, 2 * last + 1, z0o.at[last])
-    build(1, 2 * last + 1, z1o)
-    second = product(z0o.at[last], [(z0o.at[last], low), (z1o, heights[1])])
-    arrive(2)
-    stats(2)
-    build(2, 0, z2e)
-    add_near(first + second)
+    lax.fori_loop(EARLY, pairs, every, 0)
     sent.append(send(0))
     sent.append(send(1))
 
     def far(h, carry):
-        first = product(z0e.at[h], [(z2e, heights[2])])
+        first = product(z0e.at[h], [(z2e, take[2])])
         build(2, 2 * h + 1, z2o)
-        second = product(z0o.at[h], [(z2o, heights[2])])
+        second = product(z0o.at[h], [(z2o, take[2])])
         build(2, 2 * h + 2, z2e)
         acc[2] += first + second
         return carry
 
-    lax.fori_loop(0, pairs, far, 0)
+    lax.fori_loop(0, EARLY, far, 0)
     sent.append(send(2))
 
     load_lengths.wait()
@@ -251,15 +265,17 @@
             device_id=(block, peer(d)), device_id_type=MESH)
         copy.start()
         copies.append(copy)
+    for slot in range(1, STEPS + 1):
+        sent_halo(slot)
+    for copy in [c for step in sent for c in step]:
+        copy.wait_send()
     for copy in copies:
         copy.wait_recv()
     for d in range(1, n_chan):
         best = jnp.maximum(best, peaks[d])
     out[...] = jnp.where(best > 0.5 * MASKED, best, 0.0)
 
-    sent_halo(1)
-    sent_halo(2)
-    for copy in [c for step in sent for c in step] + copies:
+    for copy in copies:
         copy.wait_send()
 
 

time: 25.1 us -> 24.2 us (0.964)
  Pallas kernels: 24.4 us -> 23.5 us
    pallas_call x1, Pallas kernels: 24.4 us -> 23.5 us  [body(): pl.pallas_call(functools.partial(kernel, n_tm, n_chan), out_shape=pltpu.V...]
where the time goes in v3:
time: 24.2 us; the launch traced here: 24.1 us
  Pallas kernels  23.5 us (97%)
  local copies, waits for them, and re-layouts  0.56 us (2%)
    pallas_call x1, Pallas kernels, body(): pl.pallas_call(functools.partial(kernel, n_tm, n_chan), out_shape=pltpu.V...  23.5 us
    unnamed x1, local copies, waits for them, and re-layouts  0.56 us

profile of v3, /device:TPU:19, one launch (start us, length us, event | category | flops | bytes accessed | tf_op | source)
XLA Modules:
  0.0 24.1 jit_solution(11132640976977922352)
XLA Ops:
  0.0 23.5 %shard_map.28 = f32[1,256]{1,0:T(1,128)S(1)} custom-call(s32[16]{0:T(128)} %lengths_in.1, f32[64,256]{1,0:T(8,128)} %series.1), custom_call_target="tpu_custom_call" | custom-call | tf_op jit(solution)/shard_map/pallas_call | solution.py:294
  23.5 0.6 %copy.4 = f32[256]{0:T(256)} copy(f32[256]{0:T(256)S(1)} %bitcast.1) | data formatting | bytes 2048

commit v4 on v3

--- a/solution.py
+++ b/solution.py
@@ -53,35 +53,37 @@
         greeted = greeted + jnp.where((target >= 0) & (target < n_tm), 1, 0)
     pl.semaphore_wait(barrier, greeted)
 
-    reach = (-1, 1, 2)
-
-    def halo_copy(slot):
+    reach = (-1, -1, 1, 2)
+    pieces = ((0, 0, depth // 2), (0, depth // 2, depth), (1, 0, depth), (2, 0, depth))
+
+    def halo_copy(i):
+        slot, lo, hi = pieces[i]
         return pltpu.make_async_remote_copy(
-            src_ref=own_x, dst_ref=halo.at[slot], send_sem=halo_send.at[slot], recv_sem=halo_recv.at[slot],
-            device_id=(block + reach[slot], part), device_id_type=MESH)
-
-    def sends(slot):
-        target = block + reach[slot]
-        return (target >= 0) & (target < n_tm)
-
-    def receives(slot):
-        origin = block - reach[slot]
-        return (origin >= 0) & (origin < n_tm)
-
-    def start_halo(slot):
-        @pl.when(sends(slot))
+            src_ref=own_x.at[lo:hi, :], dst_ref=halo.at[slot, lo:hi, :], send_sem=halo_send.at[i], recv_sem=halo_recv.at[i],
+            device_id=(block + reach[i], part), device_id_type=MESH)
+
+    def start_halo(i):
+        target = block + reach[i]
+
+        @pl.when((target >= 0) & (target < n_tm))
         def _():
-            halo_copy(slot).start()
-
-    def sent_halo(slot):
-        @pl.when(sends(slot))
+            halo_copy(i).start()
+
+    def sent_halo(i):
+        target = block + reach[i]
+
+        @pl.when((target >= 0) & (target < n_tm))
         def _():
-            halo_copy(slot).wait_send()
+            halo_copy(i).wait_send()
 
     def take_halo(slot):
-        @pl.when(receives(slot))
-        def _():
-            halo_copy(slot).wait_recv()
+        for i in range(len(pieces)):
+            if pieces[i][0] == slot:
+                origin = block - reach[i]
+
+                @pl.when((origin >= 0) & (origin < n_tm))
+                def _(i=i):
+                    halo_copy(i).wait_recv()
 
     def place(upper, lower, at):
         xt[at:at + half, :] = jnp.concatenate([upper, lower], axis=0).T
@@ -150,13 +152,14 @@
 
     load.wait()
     start_halo(0)
+    start_halo(1)
     place(own_x[:, :half], own_x[:, half:], base(0))
     pad = xt.shape[0] - ((STEPS + 2) * rows - half)
     xt[xt.shape[0] - pad:, :] = jnp.zeros((pad, lanes), jnp.float32)
     acc[...] = jnp.zeros_like(acc)
     sent_halo(0)
-    start_halo(1)
     start_halo(2)
+    start_halo(3)
     take_halo(0)
 
     def arrive(step):
@@ -265,8 +268,8 @@
             device_id=(block, peer(d)), device_id_type=MESH)
         copy.start()
         copies.append(copy)
-    for slot in range(1, STEPS + 1):
-        sent_halo(slot)
+    for i in range(1, len(pieces)):
+        sent_halo(i)
     for copy in [c for step in sent for c in step]:
         copy.wait_send()
     for copy in copies:
@@ -317,8 +320,8 @@
                 pltpu.VMEM((n_chan, 1, rows), jnp.float32),
                 pltpu.SemaphoreType.DMA,
                 pltpu.SemaphoreType.DMA,
-                pltpu.SemaphoreType.DMA((STEPS + 1,)),
-                pltpu.SemaphoreType.DMA((STEPS + 1,)),
+                pltpu.SemaphoreType.DMA((STEPS + 2,)),
+                pltpu.SemaphoreType.DMA((STEPS + 2,)),
                 pltpu.SemaphoreType.DMA((STEPS + 1, n_chan - 1)),
                 pltpu.SemaphoreType.DMA((STEPS + 1, n_chan - 1)),
                 pltpu.SemaphoreType.DMA((n_chan - 1,)),

time: 24.2 us -> 23.9 us (0.988)
  the two profiles are of different devices: /device:TPU:19 before, /device:TPU:0 now
where the time goes in v4:
time: 23.9 us; the launch traced here: 23.7 us
  Pallas kernels  23.2 us (97%)
  local copies, waits for them, and re-layouts  0.56 us (2%)
    pallas_call x1, Pallas kernels, body(): pl.pallas_call(functools.partial(kernel, n_tm, n_chan), out_shape=pltpu.V...  23.2 us
    unnamed x1, local copies, waits for them, and re-layouts  0.56 us

profile of v4, /device:TPU:0, one launch (start us, length us, event | category | flops | bytes accessed | tf_op | source)
XLA Modules:
  0.0 23.7 jit_solution(2277154723009885230)
XLA Ops:
  0.0 23.2 %shard_map.28 = f32[1,256]{1,0:T(1,128)S(1)} custom-call(s32[16]{0:T(128)} %lengths_in.1, f32[64,256]{1,0:T(8,128)} %series.1), custom_call_target="tpu_custom_call" | custom-call | tf_op jit(solution)/shard_map/pallas_call | solution.py:297
  23.2 0.6 %copy.4 = f32[256]{0:T(256)} copy(f32[256]{0:T(256)S(1)} %bitcast.1) | data formatting | bytes 2048

commit v5 on v4

--- a/solution.py
+++ b/solution.py
@@ -54,7 +54,7 @@
     pl.semaphore_wait(barrier, greeted)
 
     reach = (-1, -1, 1, 2)
-    pieces = ((0, 0, depth // 2), (0, depth // 2, depth), (1, 0, depth), (2, 0, depth))
+    pieces = ((0, 0, depth // 4), (0, depth // 4, depth), (1, 0, depth), (2, 0, depth))
 
     def halo_copy(i):
         slot, lo, hi = pieces[i]
@@ -270,16 +270,13 @@
         copies.append(copy)
     for i in range(1, len(pieces)):
         sent_halo(i)
-    for copy in [c for step in sent for c in step]:
+    for copy in [c for step in sent for c in step] + copies:
         copy.wait_send()
     for copy in copies:
         copy.wait_recv()
     for d in range(1, n_chan):
         best = jnp.maximum(best, peaks[d])
     out[...] = jnp.where(best > 0.5 * MASKED, best, 0.0)
-
-    for copy in copies:
-        copy.wait_send()
 
 
 def solution(mesh):

time: 23.9 us -> 23.9 us (level)
  no operation moved by 1% of the time
where the time goes in v5:
time: 23.9 us; the launch traced here: 23.7 us
  Pallas kernels  23.2 us (97%)
  local copies, waits for them, and re-layouts  0.56 us (2%)
    pallas_call x1, Pallas kernels, body(): pl.pallas_call(functools.partial(kernel, n_tm, n_chan), out_shape=pltpu.V...  23.2 us
    unnamed x1, local copies, waits for them, and re-layouts  0.56 us

profile of v5, /device:TPU:0, one launch (start us, length us, event | category | flops | bytes accessed | tf_op | source)
XLA Modules:
  0.0 23.7 jit_solution(10760963863593821888)
XLA Ops:
  0.0 23.2 %shard_map.28 = f32[1,256]{1,0:T(1,128)S(1)} custom-call(s32[16]{0:T(128)} %lengths_in.1, f32[64,256]{1,0:T(8,128)} %series.1), custom_call_target="tpu_custom_call" | custom-call | tf_op jit(solution)/shard_map/pallas_call | solution.py:294
  23.2 0.6 %copy.4 = f32[256]{0:T(256)} copy(f32[256]{0:T(256)S(1)} %bitcast.1) | data formatting | bytes 2048
